TPU v7x, 32 devices: a whole 2x2x4 slice. The times are simulated.
32 devices in a mesh: row: 4 (over y, x), col: 8 (over z, core).
Axes of the slice: x: 2, y: 2, z: 4, core: 2. Of those that a mesh axis runs over, the one named last changes fastest.
Arguments:
- mlp_param: float32 [6144, 24576], P('row', 'col'), may hold values from -250 to 250
- mlp_grad: bfloat16 [6144, 24576], P('row', 'col'), may hold values from -250 to 250
- mlp_row_state: float32 [6144], P('row'), may hold values from 0.03 to 2.7
- mlp_col_state: float32 [24576], P('col'), may hold values from 0.02 to 0.3
- attn_param: float32 [6144, 6144], P('row', 'col'), may hold values from -250 to 250
- attn_grad: bfloat16 [6144, 6144], P('row', 'col'), may hold values from -250 to 250
- attn_row_state: float32 [6144], P('row'), may hold values from 0.03 to 2.7
- attn_col_state: float32 [6144], P('col'), may hold values from 0.02 to 0.3
Outputs:
- mlp_param_new: float32 [6144, 24576], P('row', 'col')
- attn_param_new: float32 [6144, 6144], P('row', 'col')
- mlp_row_new: float32 [6144], P('row')
- mlp_col_new: float32 [24576], P('col')
- attn_row_new: float32 [6144], P('row')
- attn_col_new: float32 [6144], P('col')
- attn_copy: bfloat16 [6144, 6144], P(None, 'col')
All inputs are finite; a program needn't handle non-finite values.
Results may differ from a plain program's by a relative error of at most 0.0004.
Values may be sent and summed in bfloat16 or wider, within the bound.
A program may use at most 128 MiB of HBM per device.

v0:
```python
import jax
import jax.numpy as jnp
from jax import lax
from jax.sharding import PartitionSpec as P

STEP = 4


TINY_SQUARE = 1e-30
LEARN_RATE = 0.05
DECAY_POWER = 0.8


def local(
    mlp_param,
    mlp_grad,
    mlp_row_state,
    mlp_col_state,
    attn_param,
    attn_grad,
    attn_row_state,
    attn_col_state,
):
    keep_rate = 1.0 - STEP ** (-DECAY_POWER)
    block_rows = mlp_grad.shape[0]
    rows_total = block_rows * lax.axis_size("row")
    mlp_width = mlp_grad.shape[1] * lax.axis_size("col")
    attn_width = attn_grad.shape[1] * lax.axis_size("col")
    mlp_count = float(rows_total * mlp_width)
    attn_count = float(rows_total * attn_width)
    mlp_square = jnp.square(mlp_grad.astype(jnp.float32)) + TINY_SQUARE
    attn_square = jnp.square(attn_grad.astype(jnp.float32)) + TINY_SQUARE
    param_local = (jnp.sum(jnp.square(mlp_param)), jnp.sum(jnp.square(attn_param)))
    param_mlp, param_attn = lax.psum((param_local[0], param_local[1]), ("row", "col"))
    row_mlp, row_attn = lax.psum((jnp.sum(mlp_square, axis=1), jnp.sum(attn_square, axis=1)), "col")
    mlp_rows_new = keep_rate * mlp_row_state + (1.0 - keep_rate) * (row_mlp / mlp_width)
    attn_rows_new = keep_rate * attn_row_state + (1.0 - keep_rate) * (row_attn / attn_width)
    col_mlp, col_attn = lax.psum((jnp.sum(mlp_square, axis=0), jnp.sum(attn_square, axis=0)), "row")
    mlp_cols_new = keep_rate * mlp_col_state + (1.0 - keep_rate) * (col_mlp / rows_total)
    attn_cols_new = keep_rate * attn_col_state + (1.0 - keep_rate) * (col_attn / rows_total)
    mlp_raw = mlp_grad.astype(jnp.float32) / jnp.sqrt(mlp_rows_new[:, None] * mlp_cols_new[None, :])
    attn_raw = attn_grad.astype(jnp.float32) / jnp.sqrt(
        attn_rows_new[:, None] * attn_cols_new[None, :]
    )
    clip_local = (jnp.sum(jnp.square(mlp_raw)), jnp.sum(jnp.square(attn_raw)))
    clip_mlp, clip_attn = lax.psum((clip_local[0], clip_local[1]), ("row", "col"))
    mlp_clip = jnp.maximum(1.0, jnp.sqrt(clip_mlp / mlp_count))
    attn_clip = jnp.maximum(1.0, jnp.sqrt(clip_attn / attn_count))
    mlp_step = LEARN_RATE * jnp.sqrt(param_mlp / mlp_count)
    attn_step = LEARN_RATE * jnp.sqrt(param_attn / attn_count)
    mlp_new = mlp_param - mlp_step * (mlp_raw / mlp_clip)
    attn_new = attn_param - attn_step * (attn_raw / attn_clip)
    weight_copy = lax.all_gather(attn_new.astype(jnp.bfloat16), "row", axis=0, tiled=True)
    return (
        mlp_new,
        attn_new,
        mlp_rows_new,
        mlp_cols_new,
        attn_rows_new,
        attn_cols_new,
        weight_copy,
    )


def solution(mesh):
    return jax.shard_map(
        local,
        mesh=mesh,
        in_specs=(
            P("row", "col"),
            P("row", "col"),
            P("row"),
            P("col"),
            P("row", "col"),
            P("row", "col"),
            P("row"),
            P("col"),
        ),
        out_specs=(
            P("row", "col"),
            P("row", "col"),
            P("row"),
            P("col"),
            P("row"),
            P("col"),
            P(None, "col"),
        ),
        check_vma=False,
    )
```

profile of v0, /device:TPU:0, one launch (start us, length us, event | category | flops | bytes accessed | tf_op | source)
XLA Modules:
  0.0 249.6 jit_solution(1990881381430585324)
XLA Ops:
  7.2 0.0 copy-start
  7.2 0.0 all-gather.2.cloned.1.call-start
  7.2 12.0 %multiply_reduce_fusion.1 = f32[]{:T(128)} fusion(f32[1536,3072]{1,0:T(8,128)} %param.8), kind=kLoop, calls=%fused_computation.7 | loop fusion | flops 9437183 | bytes 18874372 | tf_op jit(solution)/shard_map/reduce_sum | solution.py:33
  19.2 0.0 copy-done
  19.2 0.0 copy-start.5
  19.2 0.0 copy-start.6
  19.2 0.0 copy-start.7
  19.2 1.0 fusion.5
  20.2 0.0 copy-start.8
  20.2 0.0 slice-start
  20.2 13.0 %fusion.2 = (f32[1536]{0:T(1024)S(1)}, f32[3072]{0:T(1024)S(1)}) fusion(bf16[1536,3072]{1,0:T(8,128)(2,1)} %param.9), kind=kLoop, calls=%fused_computation.4 | loop fusion | flops 23588352 | bytes 9455616 | tf_op jit(solution)/shard_map/reduce_sum | solution.py:35
  33.2 30.3 %all-reduce.1 = (f32[1536]{0:T(1024)S(1)}, f32[1536]{0:T(1024)S(1)}) all-reduce(f32[1536]{0:T(1024)S(1)} %get-tuple-element.7, f32[1536]{0:T(1024)S(1)} %get-tuple-element.9), channel_id=1, replica_groups=mesh['row'=4,'col'=8] {'col'}, use_global_device_ids=true, to_apply=%region_3.0 | all-reduce | flops 3072 | bytes 24576 | tf_op jit(solution)/shard_map/psum | solution.py:35
  63.5 16.0 %all-reduce.2 = (f32[3072]{0:T(1024)S(1)}, f32[768]{0:T(1024)S(1)}) all-reduce(f32[3072]{0:T(1024)S(1)} %get-tuple-element.8, f32[768]{0:T(1024)S(1)} %get-tuple-element.10), channel_id=1, replica_groups=mesh['row'=4,'col'=8] {'row'}, use_global_device_ids=true, to_apply=%region_5.0 | all-reduce | flops 3840 | bytes 30720 | tf_op jit(solution)/shard_map/psum | solution.py:38
  79.6 0.0 copy-done.5
  79.6 0.0 copy-start.1
  79.6 0.0 copy-done.6
  79.6 0.0 copy-done.7
  79.6 0.0 copy-start.2
  79.6 0.0 copy-start.3
  79.7 0.0 slice-start.1
  79.7 9.5 %multiply_reduce_fusion = f32[]{:T(128)} fusion(bf16[1536,3072]{1,0:T(8,128)(2,1)} %param.9, f32[3072]{0:T(1024)S(1)} %multiply_add_fusion, f32[1536]{0:T(1024)S(1)} %get-tuple-element.32), kind=kLoop, calls=%fused_computation.6 | loop fusion | flops 23592960 | bytes 9455620 | tf_op jit(solution)/shard_map/reduce_sum | solution.py:45
  89.2 0.0 copy-done.8
  89.2 0.0 copy-start.4
  89.2 2.5 %multiply_reduce_fusion.2 = f32[]{:T(128)} fusion(bf16[1536,768]{1,0:T(8,128)(2,1)S(1)} %copy-done, f32[768]{0:T(1024)S(1)} %multiply_add_fusion.3, f32[1536]{0:T(1024)S(1)} %get-tuple-element.34), kind=kLoop, calls=%fused_computation.14 | loop fusion | flops 5898239 | bytes 2368516 | tf_op jit(solution)/shard_map/reduce_sum | solution.py:45
  91.7 0.0 slice-done
  91.7 0.0 slice-done.1
  91.7 1.9 multiply_reduce_fusion.3
  93.6 37.2 %all-reduce = (f32[]{:T(128)}, f32[]{:T(128)}, f32[]{:T(128)}, f32[]{:T(128)}) all-reduce(f32[]{:T(128)} %multiply_reduce_fusion, f32[]{:T(128)} %multiply_reduce_fusion.1, f32[]{:T(128)} %multiply_reduce_fusion.2, f32[]{:T(128)} %multiply_reduce_fusion.3), channel_id=1, replica_groups=mesh['row'=4,'col'=8] {'row','col'}, use_global_device_ids=true, to_apply=%region_7.0 | all-reduce | flops 4 | bytes 32 | tf_op jit(solution)/shard_map/psum | solution.py:46
  132.3 5.4 %fusion.6 = (bf16[1536,768]{1,0:T(8,128)(2,1)}, f32[1536,768]{1,0:T(8,128)}) fusion(f32[1536,768]{1,0:T(8,128)} %param.12, f32[]{:T(128)S(6)} %max.7, f32[768]{0:T(1024)S(1)} %multiply_add_fusion.3, f32[1536]{0:T(1024)S(1)} %get-tuple-element.34, bf16[1536,768]{1,0:T(8,128)(2,1)S(1)} %copy-done, f32[]{:T(128)S(6)} %mul.97), kind=kLoop, calls=%fused_computation.20 | loop fusion | flops 8257536 | bytes 14165000 | tf_op jit(solution)/shard_map/convert_element_type | solution.py:53
  137.7 0.0 copy-done.2
  137.7 0.0 copy-done.4
  137.7 0.0 all-gather.2.cloned.1.call-update
  139.1 0.0 copy-done.1
  139.1 0.0 copy-done.3
  139.1 19.4 %multiply_subtract_fusion = f32[1536,3072]{1,0:T(8,128)} fusion(f32[1536,3072]{1,0:T(8,128)} %param.8, bf16[1536,3072]{1,0:T(8,128)(2,1)} %param.9, f32[]{:T(128)S(6)} %max.6, f32[3072]{0:T(1024)S(1)} %multiply_add_fusion, f32[1536]{0:T(1024)S(1)} %get-tuple-element.32, f32[]{:T(128)S(6)} %mul.84), kind=kLoop, calls=%fused_computation.5 | loop fusion | flops 28311552 | bytes 47204360 | tf_op jit(solution)/shard_map/sub | solution.py:51
  158.5 76.3 %all-gather.2.cloned.1.call-done = bf16[6144,768]{1,0:T(8,128)(2,1)} async-done(((bf16[1536,768]{1,0:T(8,128)(2,1)}), bf16[6144,768]{1,0:T(8,128)(2,1)}) %all-gather.2.cloned.1.call-update) | async-done | bytes 9437200 | tf_op jit(solution)/shard_map/all_gather | solution.py:53
  234.8 8.0 %copy.16 = bf16[6144,768]{1,0:T(8,128)(2,1)} copy(bf16[6144,768]{1,0:T(8,128)(2,1)} %all-gather.2.cloned.1.call-done) | data formatting | bytes 18874368
  (4 shorter events, 0.0 us)
Async XLA Ops:
  7.2 12.0 %copy-start = (bf16[1536,768]{1,0:T(8,128)(2,1)S(1)}, bf16[1536,768]{1,0:T(8,128)(2,1)}, u32[]{:S(2)}) copy-start(bf16[1536,768]{1,0:T(8,128)(2,1)} %param.13) | copy-start | bytes 7077892
  7.2 227.6 %all-gather.2.cloned.1.call-start = ((), (), s32[]{:S(2)}) async-start(), calls=%async_computation | async-start | bytes 11796480 | tf_op jit(solution)/shard_map/all_gather | solution.py:53
  19.2 60.4 %copy-start.5 = (f32[3072]{0:T(1024)S(1)}, f32[3072]{0:T(1024)}, u32[]{:S(2)}) copy-start(f32[3072]{0:T(1024)} %param.11) | copy-start | bytes 36868
  19.2 60.4 %copy-start.6 = (f32[1536]{0:T(1024)S(1)}, f32[1536]{0:T(1024)}, u32[]{:S(2)}) copy-start(f32[1536]{0:T(1024)} %param.14) | copy-start | bytes 18436
  19.2 60.4 %copy-start.7 = (f32[1536]{0:T(1024)S(1)}, f32[1536]{0:T(1024)}, u32[]{:S(2)}) copy-start(f32[1536]{0:T(1024)} %param.10) | copy-start | bytes 18436
  20.2 69.0 %copy-start.8 = (f32[768]{0:T(1024)S(1)}, f32[768]{0:T(1024)}, u32[]{:S(2)}) copy-start(f32[768]{0:T(1024)} %param.15) | copy-start | bytes 9220
  20.2 71.5 %slice-start = ((s8[4718592]{0:T(1024)(128)(4,1)}), s8[524288]{0:T(1024)(128)(4,1)S(1)}, s32[]{:S(2)}) async-start(s8[4718592]{0:T(1024)(128)(4,1)} %bitcast), calls=%async_computation.1 | async-start | bytes 1048576
  79.6 59.5 %copy-start.1 = (f32[3072]{0:T(1024)}, f32[3072]{0:T(1024)S(1)}, u32[]{:S(2)}) copy-start(f32[3072]{0:T(1024)S(1)} %multiply_add_fusion) | copy-start | bytes 36868
  79.6 58.1 %copy-start.2 = (f32[1536]{0:T(1024)}, f32[1536]{0:T(1024)S(1)}, u32[]{:S(2)}) copy-start(f32[1536]{0:T(1024)S(1)} %get-tuple-element.34) | copy-start | bytes 18436
  79.6 59.5 %copy-start.3 = (f32[1536]{0:T(1024)}, f32[1536]{0:T(1024)S(1)}, u32[]{:S(2)}) copy-start(f32[1536]{0:T(1024)S(1)} %get-tuple-element.32) | copy-start | bytes 18436
  79.7 12.1 %slice-start.1 = ((s8[4718592]{0:T(1024)(128)(4,1)}), s8[4194304]{0:T(1024)(128)(4,1)S(1)}, s32[]{:S(2)}) async-start(s8[4718592]{0:T(1024)(128)(4,1)} %bitcast), calls=%async_computation.2 | async-start | bytes 8388608
  89.2 48.5 %copy-start.4 = (f32[768]{0:T(1024)}, f32[768]{0:T(1024)S(1)}, u32[]{:S(2)}) copy-start(f32[768]{0:T(1024)S(1)} %multiply_add_fusion.3) | copy-start | bytes 9220
Sparse Core Ops, SparseCore 0:
  137.8 96.8 all-gather.1
where the time goes:
time: 250 us
  blocking collectives  83.6 us (33%)
  waiting for transfers between devices  76.3 us (31%)
  other arithmetic  64.7 us (26%)
  between operations  17 us (7%)
  local copies, waits for them, and re-layouts  8.09 us (3%)
    all_gather x1, waiting for transfers between devices, local(): lax.all_gather(attn_new.astype(jnp.bfloat16), 'row', axis=0, tiled=True)  76.3 us
    psum x1, blocking collectives, local(): lax.psum((clip_local[0], clip_local[1]), ('row', 'col'))  37.2 us
    psum x1, blocking collectives, local(): lax.psum((jnp.sum(mlp_square, axis=1), jnp.sum(attn_square, axis=1)), 'col')  30.3 us
    sub x1, other arithmetic, local(): mlp_new = mlp_param - mlp_step * (mlp_raw / mlp_clip)  19.4 us
    psum x1, blocking collectives, local(): lax.psum((jnp.sum(mlp_square, axis=0), jnp.sum(attn_square, axis=0)), 'row')  16 us
    reduce_sum x1, other arithmetic, local(): jnp.sum(mlp_square, axis=1)  13 us
    reduce_sum x2, other arithmetic, local(): clip_local = (jnp.sum(jnp.square(mlp_raw)), jnp.sum(jnp.square(attn_raw)))  12.1 us
    reduce_sum x1, other arithmetic, local(): jnp.sum(jnp.square(mlp_param))  12 us
  transfers between devices with their start and end apart: 1, of which 1 were waited for; matrix products, arithmetic and copies ran while one was open for 8% of the time, Pallas kernels for 0%

commit v1 on v0

--- a/solution.py
+++ b/solution.py
@@ -1,6 +1,10 @@
+import functools
+
 import jax
 import jax.numpy as jnp
 from jax import lax
+from jax.experimental import pallas as pl
+from jax.experimental.pallas import tpu as pltpu
 from jax.sharding import PartitionSpec as P
 
 STEP = 4
@@ -62,9 +66,377 @@
     )
 
 
+LANES = 128
+MESH = pl.DeviceIdType.MESH
+
+
+def exchange(slots, axis, sems):
+    count = slots.shape[0]
+    me = lax.axis_index(axis)
+    copies = []
+    for step in range(1, count):
+        copy = pltpu.make_async_remote_copy(
+            src_ref=slots.at[me],
+            dst_ref=slots.at[me],
+            send_sem=sems.at[0, step],
+            recv_sem=sems.at[1, step],
+            device_id={axis: lax.rem(me + step, count)},
+            device_id_type=MESH,
+        )
+        copy.start()
+        copies.append(copy)
+    return copies
+
+
+def finish(copies):
+    for copy in copies:
+        copy.wait()
+
+
+def total(slots):
+    result = slots[0]
+    for rank in range(1, slots.shape[0]):
+        result = result + slots[rank]
+    return result
+
+
+def across(row):
+    return jnp.transpose(jnp.broadcast_to(row, (LANES, LANES)))
+
+
+def fold(block):
+    result = block[:, :LANES]
+    for start in range(LANES, block.shape[1], LANES):
+        result = result + block[:, start : start + LANES]
+    return result
+
+
+class Matrix:
+    def __init__(self, grad_hbm, param_hbm, row_state, col_state, rows_new, cols_new, scratch):
+        self.grad_hbm, self.param_hbm = grad_hbm, param_hbm
+        self.row_state, self.col_state = row_state, col_state
+        self.rows_new, self.cols_new = rows_new, cols_new
+        self.grad, self.param, self.row_slots, self.col_slots, self.near_slots = scratch[:5]
+        self.load_sems, self.row_sems, self.col_sems, self.near_sems = scratch[5:]
+        self.chunks, self.width = rows_new.shape[0], cols_new.shape[1]
+
+    def load(self, place):
+        source, target = ((self.grad_hbm, self.grad), (self.param_hbm, self.param))[place]
+        height = self.chunks * LANES // LOADS
+        loads = []
+        for part in range(LOADS):
+            area = pl.ds(part * height, height)
+            load = pltpu.make_async_copy(source.at[area], target.at[area], self.load_sems.at[place, part])
+            load.start()
+            loads.append(load)
+        return loads
+
+    def sweep(self, loads, body, carry):
+        for part, load in enumerate(loads):
+            load.wait()
+            carry = lax.fori_loop(
+                part * self.chunks // LOADS, (part + 1) * self.chunks // LOADS, body, carry
+            )
+        return carry
+
+    def first(self, loads):
+        me_row, me_col = lax.axis_index("row"), lax.axis_index("col")
+
+        def body(k, cols):
+            square = jnp.square(self.grad[rows_of(k), :].astype(jnp.float32)) + TINY_SQUARE
+            sums = jnp.sum(jnp.transpose(fold(square)), axis=0, keepdims=True)
+            self.row_slots[me_col, pl.ds(k, 1), :] = sums
+            return cols + jnp.sum(square.reshape(LANES // 8, 8, self.width), axis=0)
+
+        cols = self.sweep(loads, body, jnp.zeros((8, self.width), jnp.float32))
+        self.col_slots[me_row] = jnp.sum(cols, axis=0, keepdims=True)
+
+    def send(self):
+        return exchange(self.row_slots, "col", self.row_sems) + exchange(
+            self.col_slots, "row", self.col_sems
+        )
+
+    def powers(self, loads):
+        def body(k, acc):
+            square = fold(jnp.square(self.param[rows_of(k), :]))
+            return acc + jnp.sum(square.reshape(LANES // 8, 8, LANES), axis=0)
+
+        return self.sweep(loads, body, jnp.zeros((8, LANES), jnp.float32))
+
+    def factors(self):
+        keep_rate = 1.0 - STEP ** (-DECAY_POWER)
+        width_total = self.width * self.row_slots.shape[0]
+        rows_total = self.chunks * LANES * self.col_slots.shape[0]
+        rows, cols = total(self.row_slots) / width_total, total(self.col_slots) / rows_total
+        self.rows_new[...] = keep_rate * self.row_state[...] + (1.0 - keep_rate) * rows
+        self.cols_new[...] = keep_rate * self.col_state[...] + (1.0 - keep_rate) * cols
+
+    def raws(self):
+        col_inverse = 1.0 / self.cols_new[...]
+
+        def body(k, acc):
+            square = jnp.square(self.grad[rows_of(k), :].astype(jnp.float32))
+            part = fold(square * col_inverse) * across(1.0 / self.rows_new[pl.ds(k, 1), :])
+            return acc + jnp.sum(part.reshape(LANES // 8, 8, LANES), axis=0)
+
+        return lax.fori_loop(0, self.chunks, body, jnp.zeros((8, LANES), jnp.float32))
+
+    def near(self, raws, powers):
+        self.near_slots[lax.axis_index("col")] = jnp.concatenate(
+            [jnp.broadcast_to(jnp.sum(v, axis=0, keepdims=True), (4, LANES)) for v in (raws, powers)],
+            axis=0,
+        )
+        return exchange(self.near_slots, "col", self.near_sems)
+
+
+def rows_of(k):
+    return pl.ds(pl.multiple_of(k * LANES, LANES), LANES)
+
+
+def greet(axes):
+    barrier = pltpu.get_barrier_semaphore()
+    answers = 0
+    for axis, size in axes:
+        me = lax.axis_index(axis)
+        for step in range(1, size):
+            peer = {axis: lax.rem(me + step, size)}
+            pl.semaphore_signal(barrier, inc=1, device_id=peer, device_id_type=MESH)
+        answers += size - 1
+    return answers
+
+
+def factor_of(far_slots, count):
+    sums = jnp.sum(total(far_slots), axis=1, keepdims=True)
+    clip = jnp.maximum(1.0, jnp.sqrt(sums[0:1] / count))
+    step_size = LEARN_RATE * jnp.sqrt(sums[4:5] / count)
+    return jnp.broadcast_to(step_size / clip, (1, LANES))
+
+
+def stats_kernel(attn_count, mlp_count, *refs):
+    ins, outs, scratch = refs[:8], refs[8:16], refs[16:]
+    attn = Matrix(*ins[:4], *outs[:2], scratch[:9])
+    mlp = Matrix(*ins[4:], *outs[2:4], scratch[9:18])
+    coef, low, high, mlp_coef = outs[4:]
+    far_slots, far_sems, mlp_far_slots, mlp_far_sems = scratch[18:]
+    me_row = lax.axis_index("row")
+    ncol, nrow = attn.row_slots.shape[0], attn.col_slots.shape[0]
+
+    attn_grads = attn.load(0)
+    attn_params = attn.load(1)
+    answers = greet((("col", ncol), ("row", nrow)))
+    mlp_grads = mlp.load(0)
+    attn.first(attn_grads)
+    pl.semaphore_wait(pltpu.get_barrier_semaphore(), answers)
+    attn_sends = attn.send()
+    mlp_params = mlp.load(1)
+    mlp.first(mlp_grads)
+    mlp_sends = mlp.send()
+    attn_powers = attn.powers(attn_params)
+    finish(attn_sends)
+    attn.factors()
+    attn_near = attn.near(attn.raws(), attn_powers)
+    mlp_powers = mlp.powers(mlp_params)
+    finish(attn_near)
+    far_slots[me_row] = total(attn.near_slots)
+    far = exchange(far_slots, "row", far_sems)
+    finish(mlp_sends)
+    mlp.factors()
+    near = mlp.near(mlp.raws(), mlp_powers)
+    finish(far)
+    factor = factor_of(far_slots, attn_count)
+    coef[...] = factor
+    col_root = lax.rsqrt(attn.cols_new[...])
+    half_chunks = attn.chunks // 2
+    for number, half in enumerate((low, high)):
+
+        def update(k, carry):
+            place = number * half_chunks + k
+            row_root = across(factor * lax.rsqrt(attn.rows_new[pl.ds(place, 1), :]))
+            for start in range(0, attn.width, LANES):
+                lanes = pl.ds(start, LANES)
+                raw = attn.grad[rows_of(place), lanes].astype(jnp.float32) * row_root
+                fresh = attn.param[rows_of(place), lanes] - raw * col_root[:, start : start + LANES]
+                half[rows_of(k), lanes] = fresh.astype(jnp.bfloat16)
+            return carry
+
+        lax.fori_loop(0, half_chunks, update, 0)
+        if number == 0:
+            finish(near)
+            mlp_far_slots[me_row] = total(mlp.near_slots)
+            far = exchange(mlp_far_slots, "row", mlp_far_sems)
+    finish(far)
+    mlp_coef[...] = factor_of(mlp_far_slots, mlp_count)
+
+
+LOADS = 2
+
+
+def stats(attn, mlp, nrow, ncol):
+    f32 = jnp.float32
+    whole = pl.BlockSpec(memory_space=pltpu.VMEM)
+    away = pl.BlockSpec(memory_space=pltpu.HBM)
+    dma = pltpu.SemaphoreType.DMA
+    operands, shapes, scratch = [], [], []
+    for param, grad, row_state, col_state in (attn, mlp):
+        rows, width = grad.shape
+        chunks = rows // LANES
+        operands += [grad, param, row_state.reshape(chunks, LANES), col_state.reshape(1, width)]
+        shapes += [jax.ShapeDtypeStruct((chunks, LANES), f32), jax.ShapeDtypeStruct((1, width), f32)]
+        scratch += [
+            pltpu.VMEM((rows, width), grad.dtype),
+            pltpu.VMEM((rows, width), f32),
+            pltpu.VMEM((ncol, chunks, LANES), f32),
+            pltpu.VMEM((nrow, 1, width), f32),
+            pltpu.VMEM((ncol, 8, LANES), f32),
+            dma((2, LOADS)),
+            dma((2, ncol)),
+            dma((2, nrow)),
+            dma((2, ncol)),
+        ]
+    rows, width = attn[1].shape
+    shapes += [jax.ShapeDtypeStruct((1, LANES), f32)]
+    shapes += [jax.ShapeDtypeStruct((rows // 2, width), jnp.bfloat16)] * 2
+    shapes += [jax.ShapeDtypeStruct((1, LANES), f32)]
+    scratch += [pltpu.VMEM((nrow, 8, LANES), f32), dma((2, nrow))] * 2
+    counts = [float(m[1].size * nrow * ncol) for m in (attn, mlp)]
+    return pl.pallas_call(
+        functools.partial(stats_kernel, *counts),
+        out_shape=shapes,
+        in_specs=[away, away, whole, whole] * 2,
+        out_specs=[whole] * len(shapes),
+        scratch_shapes=scratch,
+        compiler_params=pltpu.CompilerParams(
+            collective_id=0, has_side_effects=True, vmem_limit_bytes=VMEM_BYTES
+        ),
+        cost_estimate=pl.CostEstimate(
+            flops=8 * mlp[1].size, bytes_accessed=8 * mlp[1].size, transcendentals=0
+        ),
+    )(*operands)
+
+
+VMEM_BYTES = 66_900_000
+PARTS = 4
+
+
+def place_kernel(picks, masks, extra, *refs):
+    count = len(masks)
+    pieces, held, sems = refs[:count], refs[-2], refs[-1]
+    out, copies = refs[-3 - extra], refs[len(refs) - 2 - extra : -2]
+    originals = refs[len(refs) - 3 - 2 * extra : len(refs) - 3 - extra]
+    me = lax.axis_index("row")
+    rows = held.shape[1]
+    size = rows // PARTS
+    parts = [(i, part) for i in range(count) for part in range(PARTS)]
+    loads = []
+    for i, part in parts:
+        area = pl.ds(part * size, size)
+        load = pltpu.make_async_copy(pieces[i].at[area], held.at[i, area], sems.at[0, i, part])
+        load.start()
+        loads.append(load)
+    for original, duplicate in zip(originals, copies):
+        duplicate[...] = original[...]
+    stores = []
+    for (i, part), load in zip(parts, loads):
+        bit_x, bit_y = lax.rem(me, 2), lax.div(me, 2)
+        if masks[i] & 1:
+            bit_x = 1 - bit_x
+        if masks[i] & 2:
+            bit_y = 1 - bit_y
+        start = ((bit_y * 2 + bit_x) * 2 + picks[i]) * rows + part * size
+        load.wait()
+        store = pltpu.make_async_copy(
+            held.at[i, pl.ds(part * size, size)],
+            out.at[pl.ds(pl.multiple_of(start, size), size)],
+            sems.at[1, i, part],
+        )
+        store.start()
+        stores.append(store)
+    for store in stores:
+        store.wait()
+
+
+def place(pieces, picks, masks, base, vectors):
+    rows, width = pieces[0].shape
+    count = len(pieces)
+    away = pl.BlockSpec(memory_space=pl.ANY)
+    whole = pl.BlockSpec(memory_space=pltpu.VMEM)
+    operands = list(pieces) + ([] if base is None else [base])
+    return pl.pallas_call(
+        functools.partial(place_kernel, picks, masks, len(vectors)),
+        out_shape=[jax.ShapeDtypeStruct((8 * rows, width), pieces[0].dtype)]
+        + [jax.ShapeDtypeStruct(v.shape, v.dtype) for v in vectors],
+        in_specs=[away] * len(operands) + [whole] * len(vectors),
+        out_specs=[away] + [whole] * len(vectors),
+        input_output_aliases={} if base is None else {count: 0},
+        scratch_shapes=[
+            pltpu.VMEM((count, rows, width), pieces[0].dtype),
+            pltpu.SemaphoreType.DMA((2, count, PARTS)),
+        ],
+        cost_estimate=pl.CostEstimate(
+            flops=0, bytes_accessed=4 * count * rows * width, transcendentals=0
+        ),
+    )(*operands, *vectors)
+
+
+def root_of(rows_new, coef):
+    return coef[0, 0] * lax.rsqrt(rows_new.reshape(-1))
+
+
+def updated(param, grad, row_root, cols_new):
+    return param - (grad.astype(jnp.float32) * row_root[:, None]) * lax.rsqrt(cols_new.reshape(-1))[None, :]
+
+
+def local_fast(
+    nrow,
+    ncol,
+    mlp_param,
+    mlp_grad,
+    mlp_row_state,
+    mlp_col_state,
+    attn_param,
+    attn_grad,
+    attn_row_state,
+    attn_col_state,
+):
+    attn_rows, attn_cols, mlp_rows, mlp_cols, attn_coef, low, high, mlp_coef = stats(
+        (attn_param, attn_grad, attn_row_state, attn_col_state),
+        (mlp_param, mlp_grad, mlp_row_state, mlp_col_state),
+        nrow,
+        ncol,
+    )
+    over_x = [(i, i ^ 1) for i in range(4)]
+    over_y = [(i, i ^ 2) for i in range(4)]
+    x_high = lax.ppermute(high, "row", over_x)
+    y_low = lax.ppermute(low, "row", over_y)
+    mlp_root, low_late, high_late = lax.optimization_barrier((root_of(mlp_rows, mlp_coef), low, high))
+    x_low = lax.ppermute(low_late, "row", over_x)
+    y_high = lax.ppermute(high_late, "row", over_y)
+    mlp_new = updated(mlp_param, mlp_grad, mlp_root, mlp_cols)
+    mlp_new, x_high, y_low = lax.optimization_barrier((mlp_new, x_high, y_low))
+    far_low = lax.ppermute(y_low, "row", over_x)
+    far_high = lax.ppermute(x_high, "row", over_y)
+    factors = (mlp_rows, mlp_cols, attn_rows, attn_cols)
+    copy, *factors = place((low, high, x_high, y_low), (0, 1, 1, 0), (0, 0, 1, 2), None, factors)
+    mlp_rows, mlp_cols, attn_rows, attn_cols = (v.reshape(-1) for v in factors)
+    attn_new = updated(attn_param, attn_grad, root_of(attn_rows, attn_coef), attn_cols)
+    (copy,) = place((x_low, y_high), (0, 1), (1, 2), copy, ())
+    (copy,) = place((far_low, far_high), (0, 1), (3, 3), copy, ())
+    return (mlp_new, attn_new, mlp_rows, mlp_cols, attn_rows, attn_cols, copy)
+
+
 def solution(mesh):
+    nrow, ncol = mesh.shape["row"], mesh.shape["col"]
+
+    def step(*args):
+        aligned = all(
+            a.shape[0] % (4 * LANES) == 0 and a.shape[1] % LANES == 0 for a in (args[0], args[4])
+        )
+        if nrow == 4 and ncol > 1 and aligned and 6 * (args[0].size + args[4].size) <= VMEM_BYTES * 3 // 4:
+            return local_fast(nrow, ncol, *args)
+        return local(*args)
+
     return jax.shard_map(
-        local,
+        step,
         mesh=mesh,
         in_specs=(
             P("row", "col"),

time: 250 us -> 114 us (0.46)
  blocking collectives: 83.6 us -> 0 us
  Pallas kernels: 0 us -> 41.5 us
  waiting for transfers between devices: 76.3 us -> 36.2 us
  other arithmetic: 64.7 us -> 24.8 us
  between operations: 17 us -> 0.7 us
  starting transfers between devices: 0.04 us -> 6.15 us
  local copies, waits for them, and re-layouts: 8.09 us -> 4.07 us
    psum x3 -> x0, blocking collectives: 83.6 us -> none  [the longest x1 37.2 us: local(): lax.psum((clip_local[0], clip_local[1]), ('row', 'col'))]
    all_gather x1 -> x0, waiting for transfers between devices: 76.3 us -> none  [local(): lax.all_gather(attn_new.astype(jnp.bfloat16), 'row', axis=0, tiled=True)]
    pallas_call x0 -> x4, Pallas kernels: none -> 41.5 us  [the longest x1 30.6 us: stats(): pl.pallas_call(functools.partial(stats_kernel, *counts), out_shape=shapes...]
    reduce_sum x6 -> x0, other arithmetic: 39.9 us -> none  [the longest x1 13 us: local(): jnp.sum(mlp_square, axis=1)]
    ppermute x0 -> x6, waiting for transfers between devices: none -> 36.2 us  [the longest x1 16.8 us: local_fast(): x_low = lax.ppermute(low_late, 'row', over_x)]
    unnamed x23 -> x14, local copies, waits for them, and re-layouts: 8.09 us -> 1.47 us
    ppermute x0 -> x6, starting transfers between devices: none -> 6.15 us  [the longest x1 1.47 us: local_fast(): x_low = lax.ppermute(low_late, 'row', over_x)]
    convert_element_type x1 -> x0, other arithmetic: 5.39 us -> none  [local(): attn_new.astype(jnp.bfloat16)]
  transfers between devices with their start and end apart: 1 -> 6, of which waited for: 1 -> 6; matrix products, arithmetic and copies ran while one was open for 8% -> 23% of each run, Pallas kernels for 0% -> 7%
where the time goes in v1:
time: 114 us; the launch traced here: 113 us
  Pallas kernels  41.5 us (36%)
  waiting for transfers between devices  36.2 us (32%)
  other arithmetic  24.8 us (22%)
  starting transfers between devices  6.15 us (5%)
  local copies, waits for them, and re-layouts  4.07 us (4%)
    pallas_call x1, Pallas kernels, stats(): pl.pallas_call(functools.partial(stats_kernel, *counts), out_shape=shapes...  30.6 us
    sub x2, other arithmetic, updated(): param - grad.astype(jnp.float32) * row_root[:, None] * lax.rsqrt(cols_new...  23.5 us
    ppermute x1, waiting for transfers between devices, local_fast(): x_low = lax.ppermute(low_late, 'row', over_x)  16.8 us
    ppermute x1, waiting for transfers between devices, local_fast(): far_low = lax.ppermute(y_low, 'row', over_x)  13.1 us
    pallas_call x3, Pallas kernels, place(): pl.pallas_call(functools.partial(place_kernel, picks, masks, len(vectors)...  10.9 us
    ppermute x1, waiting for transfers between devices, local_fast(): x_high = lax.ppermute(high, 'row', over_x)  4.73 us
  transfers between devices with their start and end apart: 6, of which 6 were waited for; matrix products, arithmetic and copies ran while one was open for 23% of the time, Pallas kernels for 7%

profile of v1, /device:TPU:0, one launch (start us, length us, event | category | flops | bytes accessed | tf_op | source)
XLA Modules:
  0.0 113.4 jit_solution(10691831493097841982)
XLA Ops:
  0.6 1.3 %reshape.51.refs_3_ = f32[1,768]{1,0:T(1,128)} reshape(f32[768]{0:T(1024)} %param.15) | data formatting | bytes 6144 | tf_op jit(solution)/shard_map/reshape | solution.py:283
  1.9 30.6 %shard_map.135 = (f32[12,128]{1,0:T(8,128)}, f32[1,768]{1,0:T(1,128)}, f32[12,128]{1,0:T(8,128)}, f32[1,3072]{1,0:T(1,128)}, f32[1,128]{1,0:T(1,128)}, /*index=5...) custom-call(bf16[1536,768]{1,0:T(8,128)(2,1)} %refs_0_.1, f32[1536,768]{1,0:T(8,128)} %refs_1_.1, ...), custom_call_target="tpu_custom_call" | custom-call | flops 37748736 | bytes 37748736 | tf_op jit(solution)/shard_map/pallas_call | solution.py:302
  32.5 0.7 collective-permute-start
  33.2 0.6 collective-permute-start.1
  33.7 1.3 %multiply_bitcast_fusion = f32[1536]{0:T(1024)S(1)} fusion(f32[12,128]{1,0:T(8,128)} %get-tuple-element.27.refs_4_, f32[]{:T(128)} %bitcast.20), kind=kLoop, calls=%fused_computation.3 | loop fusion | flops 1536 | bytes 12292 | tf_op jit(solution)/shard_map/mul | solution.py:382
  35.0 1.5 %collective-permute-start.4 = (bf16[768,768]{1,0:T(8,128)(2,1)}, bf16[768,768]{1,0:T(8,128)(2,1)S(1)}, u32[]{:S(2)}, u32[]{:S(2)}) collective-permute-start(bf16[768,768]{1,0:T(8,128)(2,1)} %get-tuple-element.42.refs_0_), channel_id=1, source_target_pairs={{0,8},{8,0},{16,24},{24,16},{1,9},{9,1},{17,25},{25,17},{2,10},{10... | collective-permute-start | bytes 3538952 | tf_op jit(solution)/shard_map/ppermute | solution.py:412
  36.5 1.4 %collective-permute-start.5 = (bf16[768,768]{1,0:T(8,128)(2,1)}, bf16[768,768]{1,0:T(8,128)(2,1)S(1)}, u32[]{:S(2)}, u32[]{:S(2)}) collective-permute-start(bf16[768,768]{1,0:T(8,128)(2,1)} %get-tuple-element.43.refs_1_), channel_id=1, source_target_pairs={{0,16},{8,24},{16,0},{24,8},{1,17},{9,25},{17,1},{25,9},{2,18},{10... | collective-permute-start | bytes 3538952 | tf_op jit(solution)/shard_map/ppermute | solution.py:413
  37.9 0.7 rsqrt.20
  38.6 18.3 %multiply_subtract_fusion = f32[1536,3072]{1,0:T(8,128)} fusion(f32[1536,3072]{1,0:T(8,128)} %refs_5_.1, bf16[1536,3072]{1,0:T(8,128)(2,1)} %refs_4_.1, f32[3072]{0:T(1024)S(1)} %bitcast.14, f32[1536]{0:T(1024)S(1)} %multiply_bitcast_fusion), kind=kLoop, calls=%fused_computation | loop fusion | flops 18874368 | bytes 47204352 | tf_op jit(solution)/shard_map/sub | solution.py:386
  56.9 4.7 %collective-permute-done.refs_2_ = bf16[768,768]{1,0:T(8,128)(2,1)S(1)} collective-permute-done((bf16[768,768]{1,0:T(8,128)(2,1)}, bf16[768,768]{1,0:T(8,128)(2,1)S(1)}, u32[]{:S(2)}, u32[]{:S(2)}) %collective-permute-start) | collective-permute-done | bytes 1179680 | tf_op jit(solution)/shard_map/ppermute | solution.py:409
  61.6 0.0 copy-start.1
  61.6 0.7 collective-permute-done.1.refs_3_
  62.3 1.4 %collective-permute-start.2 = (bf16[768,768]{1,0:T(8,128)(2,1)}, bf16[768,768]{1,0:T(8,128)(2,1)}, u32[]{:S(2)}, u32[]{:S(2)}) collective-permute-start(bf16[768,768]{1,0:T(8,128)(2,1)} %collective-permute-done.1.refs_3_), channel_id=1, source_target_pairs={{0,8},{8,0},{16,24},{24,16},{1,9},{9,1},{17,25},{25,17},{2,10},{10... | collective-permute-start | bytes 3538952 | tf_op jit(solution)/shard_map/ppermute | solution.py:416
  63.8 0.6 collective-permute-start.3
  64.4 0.0 copy-done.1
  64.4 5.7 %shard_map.136 = (bf16[6144,768]{1,0:T(8,128)(2,1)}, f32[12,128]{1,0:T(8,128)}, f32[1,3072]{1,0:T(1,128)}, f32[12,128]{1,0:T(8,128)}, f32[1,768]{1,0:T(1,128)}) custom-call(bf16[768,768]{1,0:T(8,128)(2,1)} %get-tuple-element.42.refs_0_, bf16[768,768]{1,0:T(8,128)(2,1)} %get-tuple-element.43.refs_1_, bf16[768,768]{1,0:T(8,128)(2,1)} %copy-done.1, ...), custom_call_target="tpu_custom_call" | custom-call | bytes 9437184 | tf_op jit(solution)/shard_map/pallas_call | solution.py:364
  70.1 16.8 %collective-permute-done.4.refs_0_ = bf16[768,768]{1,0:T(8,128)(2,1)S(1)} collective-permute-done((bf16[768,768]{1,0:T(8,128)(2,1)}, bf16[768,768]{1,0:T(8,128)(2,1)S(1)}, u32[]{:S(2)}, u32[]{:S(2)}) %collective-permute-start.4) | collective-permute-done | bytes 1179680 | tf_op jit(solution)/shard_map/ppermute | solution.py:412
  86.9 0.0 copy-start.2
  86.9 0.6 collective-permute-done.5.refs_1_
  87.5 0.4 copy-done.2
  87.9 0.0 copy-start.3
  87.9 1.0 copy-done.3
  89.0 0.0 copy-start.5
  89.0 0.0 copy-start.4
  89.0 0.0 copy-start.6
  89.0 0.0 copy-start
  89.0 2.6 %shard_map.137.refs_2_ = bf16[6144,768]{1,0:T(8,128)(2,1)} custom-call(bf16[768,768]{1,0:T(8,128)(2,1)} %copy-done.2, bf16[768,768]{1,0:T(8,128)(2,1)} %copy-done.3, bf16[6144,768]{1,0:T(8,128)(2,1)} %get-tuple-element.44.refs_2_), custom_call_target="tpu_custom_call", output_to_operand_aliasing={{}: (2, {})} | custom-call | bytes 4718592 | tf_op jit(solution)/shard_map/pallas_call | solution.py:364
  91.6 0.0 copy-done.5
  91.6 0.6 fusion
  92.2 0.0 copy-done.4
  92.2 0.0 copy-done.6
  92.3 0.0 copy-done
  92.3 5.2 %multiply_subtract_fusion.1 = f32[1536,768]{1,0:T(8,128)} fusion(f32[1536,768]{1,0:T(8,128)} %refs_1_.1, bf16[1536,768]{1,0:T(8,128)(2,1)S(1)} %copy-done, f32[768]{0:T(1024)S(1)} %get-tuple-element.46, f32[1536]{0:T(1024)S(1)} %rsqrt_multiply_fusion), kind=kLoop, calls=%fused_computation.1 | loop fusion | flops 4718592 | bytes 11805696 | tf_op jit(solution)/shard_map/sub | solution.py:386
  97.5 13.1 %collective-permute-done.2.refs_0_ = bf16[768,768]{1,0:T(8,128)(2,1)} collective-permute-done((bf16[768,768]{1,0:T(8,128)(2,1)}, bf16[768,768]{1,0:T(8,128)(2,1)}, u32[]{:S(2)}, u32[]{:S(2)}) %collective-permute-start.2) | collective-permute-done | bytes 1179680 | tf_op jit(solution)/shard_map/ppermute | solution.py:416
  110.6 0.3 collective-permute-done.3.refs_1_
  110.9 2.5 %shard_map.138 = bf16[6144,768]{1,0:T(8,128)(2,1)} custom-call(bf16[768,768]{1,0:T(8,128)(2,1)} %collective-permute-done.2.refs_0_, bf16[768,768]{1,0:T(8,128)(2,1)} %collective-permute-done.3.refs_1_, bf16[6144,768]{1,0:T(8,128)(2,1)} %shard_map.137.refs_2_), custom_call_target="tpu_custom_call", output_to_operand_aliasing={{}: (2, {})} | custom-call | bytes 4718592 | tf_op jit(solution)/shard_map/pallas_call | solution.py:364
  (1 shorter events, 0.0 us)
Async XLA Ops:
  32.5 29.1 %collective-permute-start = (bf16[768,768]{1,0:T(8,128)(2,1)}, bf16[768,768]{1,0:T(8,128)(2,1)S(1)}, u32[]{:S(2)}, u32[]{:S(2)}) collective-permute-start(bf16[768,768]{1,0:T(8,128)(2,1)} %get-tuple-element.43.refs_1_), channel_id=1, source_target_pairs={{0,8},{8,0},{16,24},{24,16},{1,9},{9,1},{17,25},{25,17},{2,10},{10... | collective-permute-start | bytes 3538952 | tf_op jit(solution)/shard_map/ppermute | solution.py:409
  33.2 29.2 %collective-permute-start.1 = (bf16[768,768]{1,0:T(8,128)(2,1)}, bf16[768,768]{1,0:T(8,128)(2,1)}, u32[]{:S(2)}, u32[]{:S(2)}) collective-permute-start(bf16[768,768]{1,0:T(8,128)(2,1)} %get-tuple-element.42.refs_0_), channel_id=1, source_target_pairs={{0,16},{8,24},{16,0},{24,8},{1,17},{9,25},{17,1},{25,9},{2,18},{10... | collective-permute-start | bytes 3538952 | tf_op jit(solution)/shard_map/ppermute | solution.py:410
  35.0 51.9 %collective-permute-start.4 = (bf16[768,768]{1,0:T(8,128)(2,1)}, bf16[768,768]{1,0:T(8,128)(2,1)S(1)}, u32[]{:S(2)}, u32[]{:S(2)}) collective-permute-start(bf16[768,768]{1,0:T(8,128)(2,1)} %get-tuple-element.42.refs_0_), channel_id=1, source_target_pairs={{0,8},{8,0},{16,24},{24,16},{1,9},{9,1},{17,25},{25,17},{2,10},{10... | collective-permute-start | bytes 3538952 | tf_op jit(solution)/shard_map/ppermute | solution.py:412
  36.5 51.0 %collective-permute-start.5 = (bf16[768,768]{1,0:T(8,128)(2,1)}, bf16[768,768]{1,0:T(8,128)(2,1)S(1)}, u32[]{:S(2)}, u32[]{:S(2)}) collective-permute-start(bf16[768,768]{1,0:T(8,128)(2,1)} %get-tuple-element.43.refs_1_), channel_id=1, source_target_pairs={{0,16},{8,24},{16,0},{24,8},{1,17},{9,25},{17,1},{25,9},{2,18},{10... | collective-permute-start | bytes 3538952 | tf_op jit(solution)/shard_map/ppermute | solution.py:413
  61.6 2.7 %copy-start.1 = (bf16[768,768]{1,0:T(8,128)(2,1)}, bf16[768,768]{1,0:T(8,128)(2,1)S(1)}, u32[]{:S(2)}) copy-start(bf16[768,768]{1,0:T(8,128)(2,1)S(1)} %collective-permute-done.refs_2_) | copy-start | bytes 3538948
  62.3 48.2 %collective-permute-start.2 = (bf16[768,768]{1,0:T(8,128)(2,1)}, bf16[768,768]{1,0:T(8,128)(2,1)}, u32[]{:S(2)}, u32[]{:S(2)}) collective-permute-start(bf16[768,768]{1,0:T(8,128)(2,1)} %collective-permute-done.1.refs_3_), channel_id=1, source_target_pairs={{0,8},{8,0},{16,24},{24,16},{1,9},{9,1},{17,25},{25,17},{2,10},{10... | collective-permute-start | bytes 3538952 | tf_op jit(solution)/shard_map/ppermute | solution.py:416
  63.8 47.1 %collective-permute-start.3 = (bf16[768,768]{1,0:T(8,128)(2,1)S(1)}, bf16[768,768]{1,0:T(8,128)(2,1)}, u32[]{:S(2)}, u32[]{:S(2)}) collective-permute-start(bf16[768,768]{1,0:T(8,128)(2,1)S(1)} %collective-permute-done.refs_2_), channel_id=1, source_target_pairs={{0,16},{8,24},{16,0},{24,8},{1,17},{9,25},{17,1},{25,9},{2,18},{10... | collective-permute-start | bytes 3538952 | tf_op jit(solution)/shard_map/ppermute | solution.py:417
  86.9 1.0 copy-start.2
  87.9 1.0 copy-start.3
  89.0 2.7 %copy-start.5 = (f32[1,768]{1,0:T(1,128)S(1)}, f32[1,768]{1,0:T(1,128)}, u32[]{:S(2)}) copy-start(f32[1,768]{1,0:T(1,128)} %get-tuple-element.39) | copy-start | bytes 9220
  89.0 3.3 %copy-start.4 = (f32[12,128]{1,0:T(8,128)S(1)}, f32[12,128]{1,0:T(8,128)}, u32[]{:S(2)}) copy-start(f32[12,128]{1,0:T(8,128)} %get-tuple-element.38) | copy-start | bytes 18436
  89.0 3.3 %copy-start.6 = (f32[1,128]{1,0:T(1,128)S(1)}, f32[1,128]{1,0:T(1,128)}, u32[]{:S(2)}) copy-start(f32[1,128]{1,0:T(1,128)} %get-tuple-element.33) | copy-start | bytes 1540
  89.0 3.3 %copy-start = (bf16[1536,768]{1,0:T(8,128)(2,1)S(1)}, bf16[1536,768]{1,0:T(8,128)(2,1)}, u32[]{:S(2)}) copy-start(bf16[1536,768]{1,0:T(8,128)(2,1)} %refs_0_.1) | copy-start | bytes 7077892
